TPU v7x, 32 devices: a whole 2x2x4 slice. The times are simulated.
32 devices in a mesh: dom: 8 (over z, x), sub: 4 (over y, core).
Axes of the slice: x: 2, y: 2, z: 4, core: 2. Of those that a mesh axis runs over, the one named last changes fastest.
Arguments:
- load_vector: float32 [64, 128], P(('dom', 'sub')), may hold values from -38 to 38
- recycled: float32 [40, 64, 128], P(None, ('dom', 'sub')), may hold values from -6 to 6
- images: float32 [40, 64, 128], P(None, ('dom', 'sub')), may hold values from -6 to 6
- matrix_tiles: float32 [64, 8, 128, 128], P(('dom', 'sub')), may hold values from -7 to 7
- tile_columns: int32 [64, 8], P(('dom', 'sub')), may hold values from 0 to 5, as said below
- ghost_list: int32 [32, 4], P(('dom', 'sub')), may hold values from 0 to 23, as said below
- live_counts: int32 [32], P(('dom', 'sub')), may hold values from 1 to 2, as said below
Outputs:
- solution: float32 [64, 128], P(('dom', 'sub'))
- residual: float32 [64, 128], P(('dom', 'sub'))
Inputs may be any that keep to these rules, and one draw needn't show every extreme that they name: `live_counts`: each device's live block rows are its first slots; some device has all 2 live. `tile_columns`: tile 0 of a block row names the row's own slot. Other entries below 2 name a live slot of the same device; entries from 2 on name a ghost slot of that device. `ghost_list`: each entry names a live slot q of a device with sub index s and dom index differing from the owner's by o - 1 (o of 0, 1, 2), coded as o * (size of sub) * 2 + s * 2 + q; it never points outside the dom axis and never to the owner itself.
All inputs are finite; a program needn't handle non-finite values.
Results may differ from a plain program's by a relative error of at most 0.0003.
Values sent between devices are 32-bit elements; how exact they have to be, the bound alone decides.
No kernel may reach another device: no remote copies, remote signals or barrier semaphores. Data moves between devices by JAX's collectives and lax.ppermute only.
A program may use at most 64 MiB of HBM per device.

v0:
```python
import jax
import jax.numpy as jnp
from jax import lax
from jax.sharding import PartitionSpec as P

STEPS = 3


def padded(value, sides, width):
    for axis, dim in sides:
        count, length = (lax.axis_size(axis), value.shape[dim])
        up = [(i, (i + 1) % count) for i in range(count - 1)]
        down = [(j, i) for i, j in up]
        last = lax.slice_in_dim(value, length - width, length, axis=dim)
        first = lax.slice_in_dim(value, 0, width, axis=dim)
        before = lax.ppermute(last, axis, up)
        after = lax.ppermute(first, axis, down)
        value = jnp.concatenate([before, value, after], axis=dim)
    return value


def triangle_solve(factor, values, transpose):
    column = values if values.ndim == 2 else values[:, None]
    solved = lax.linalg.triangular_solve(
        factor, column, left_side=True, lower=True, transpose_a=transpose
    )
    return solved if values.ndim == 2 else solved[:, 0]


def multiply(vector, matrix_tiles, tile_columns, ghost_codes):
    slot_count = vector.shape[0]
    group_size = lax.axis_size("sub") * slot_count
    gathered = lax.all_gather(vector, "sub", axis=0, tiled=True)
    nearby = padded(gathered, (("dom", 0),), group_size)
    ghosts = jnp.take(nearby, ghost_codes, axis=0)
    extended = jnp.concatenate([vector, ghosts], axis=0)
    picked = jnp.take(extended, tile_columns, axis=0)
    return jnp.einsum("stij,stj->si", matrix_tiles, picked, precision=lax.Precision.HIGHEST)


def local(load_vector, recycled, images, matrix_tiles, tile_columns, ghost_list, live_counts):
    highest = lax.Precision.HIGHEST
    slot_count, tile_width = load_vector.shape
    recycled_count = recycled.shape[0]
    live_mask = (jnp.arange(slot_count) < live_counts[0]).astype(jnp.float32)[:, None]
    ghost_codes = ghost_list[0]
    source = (load_vector * live_mask).reshape(-1)
    recycled_flat = (recycled * live_mask[None]).reshape(recycled_count, -1)
    images_flat = (images * live_mask[None]).reshape(recycled_count, -1)
    gram_matrix, projection, source_norm = lax.psum(
        (
            jnp.dot(images_flat, images_flat.T, precision=highest),
            jnp.dot(images_flat, source, precision=highest),
            jnp.sum(source * source),
        ),
        ("dom", "sub"),
    )
    cholesky_low = jnp.linalg.cholesky(gram_matrix)
    reduced = triangle_solve(cholesky_low, projection, False)
    initial_norm = jnp.sqrt(source_norm - jnp.sum(reduced * reduced))
    images_hat = triangle_solve(cholesky_low, images_flat, False)
    recycled_hat = triangle_solve(cholesky_low, recycled_flat, False)
    start_point = jnp.dot(reduced, recycled_hat, precision=highest)
    start_residual = source - jnp.dot(reduced, images_hat, precision=highest)
    basis = [start_residual / initial_norm]
    hessenberg = jnp.zeros((STEPS + 1, STEPS), jnp.float32)
    coupling = jnp.zeros((recycled_count, STEPS), jnp.float32)
    for column in range(STEPS):
        image_now = multiply(
            basis[column].reshape(slot_count, tile_width), matrix_tiles, tile_columns, ghost_codes
        )
        image_now = (image_now * live_mask).reshape(-1)
        stacked = jnp.stack(basis)
        local_images = jnp.dot(images_hat, image_now, precision=highest)
        summed_images, against_basis, image_norm = lax.psum(
            (
                local_images,
                jnp.dot(stacked, image_now, precision=highest),
                jnp.sum(image_now * image_now),
            ),
            ("dom", "sub"),
        )
        correction = jnp.dot(summed_images, images_hat, precision=highest)
        next_norm = jnp.sqrt(
            image_norm
            - jnp.sum(summed_images * summed_images)
            - jnp.sum(against_basis * against_basis)
        )
        remaining = image_now - correction - jnp.dot(against_basis, stacked, precision=highest)
        basis.append(remaining / next_norm)
        hessenberg = hessenberg.at[: column + 1, column].set(against_basis)
        hessenberg = hessenberg.at[column + 1, column].set(next_norm)
        coupling = coupling.at[:, column].set(summed_images)
    normal_matrix = jnp.dot(hessenberg.T, hessenberg, precision=highest)
    target = initial_norm * hessenberg[0]
    small_factor = jnp.linalg.cholesky(normal_matrix)
    least = triangle_solve(small_factor, triangle_solve(small_factor, target, False), True)
    every_basis = jnp.stack(basis)
    coupled = jnp.dot(coupling, least, precision=highest)
    recycled_term = jnp.dot(coupled, recycled_hat, precision=highest)
    solution = start_point + jnp.dot(least, every_basis[:STEPS], precision=highest) - recycled_term
    residual = start_residual - jnp.dot(
        jnp.dot(hessenberg, least, precision=highest), every_basis, precision=highest
    )
    return (solution.reshape(slot_count, tile_width), residual.reshape(slot_count, tile_width))


def solution(mesh):
    return jax.shard_map(
        local,
        mesh=mesh,
        in_specs=(
            P(("dom", "sub"), None),
            P(None, ("dom", "sub"), None),
            P(None, ("dom", "sub"), None),
            P(("dom", "sub"), None, None, None),
            P(("dom", "sub"), None),
            P(("dom", "sub"), None),
            P(("dom", "sub")),
        ),
        out_specs=(P(("dom", "sub"), None), P(("dom", "sub"), None)),
        check_vma=False,
    )
```

profile of v0, /device:TPU:0, one launch (start us, length us, event | category | flops | bytes accessed | tf_op | source)
XLA Modules:
  0.0 252.3 jit_solution(12142202452177539300)
XLA Ops:
  3.8 42.4 %all-reduce.5 = (f32[40,40]{0,1:T(8,128)S(1)}, f32[]{:T(128)}, f32[40]{0:T(128)S(1)}) all-reduce(f32[40,40]{0,1:T(8,128)S(1)} %convolution_bitcast_fusion, f32[]{:T(128)} %get-tuple-element.131, f32[40]{0:T(128)S(1)} %convolution_bitcast_fusion.5), channel_id=1, replica_groups=mesh['dom'=8,'sub'=4] {'dom','sub'}, use_global_device_ids=true, to_apply=%region_0.0 | all-reduce | flops 1641 | bytes 13128 | tf_op jit(solution)/shard_map/psum | solution.py:50
  46.3 3.6 %cholesky.29 = f32[40,40]{1,0:T(8,128)S(1)} custom-call(f32[40,40]{1,0:T(8,128)S(1)} %fusion.13), custom_call_target="Cholesky" | custom-call | tf_op jit(solution)/shard_map/jit(cholesky)/cholesky | solution.py:58
  51.3 3.1 %custom-call.17 = f32[1,40,40]{1,2,0:T(8,128)S(1)} custom-call(f32[1,40,40]{2,1,0:T(8,128)S(1)} %fusion.8), custom_call_target="InvertDiagBlocksLowerTriangular" | custom-call | tf_op jit(solution)/shard_map/triangular_solve | solution.py:24
  56.8 5.2 %all-gather = f32[4,2,128]{2,1,0:T(2,128)S(1)} all-gather(f32[1,2,128]{2,1,0:T(2,128)S(1)} %bitcast.252), channel_id=1, replica_groups=mesh['dom'=8,'sub'=4] {'sub'}, dimensions={0}, use_global_device_ids=true | all-gather | bytes 5120 | tf_op jit(solution)/shard_map/all_gather | solution.py:33
  62.0 1.4 collective-permute-start.1
  63.4 4.7 %collective-permute-start = (f32[8,128]{1,0:T(8,128)S(1)}, f32[8,128]{1,0:T(8,128)S(1)}, u32[]{:S(2)}, u32[]{:S(2)}) collective-permute-start(f32[8,128]{1,0:T(8,128)S(1)} %bitcast.262), channel_id=1, source_target_pairs={{0,4},{4,8},{8,12},{12,16},{16,20},{20,24},{24,28},{1,5},{5,9},{9,... | collective-permute-start | bytes 12296 | tf_op jit(solution)/shard_map/ppermute | solution.py:16
  72.6 1.0 fusion.61
  75.0 40.7 %all-reduce.4 = (f32[40]{0:T(128)S(1)}, f32[]{:T(128)}, f32[1]{0:T(128)}) all-reduce(f32[40]{0:T(128)S(1)} %convolution_bitcast_fusion.4, f32[]{:T(128)} %multiply_reduce_fusion.3, f32[1]{0:T(128)} %bitcast.29), channel_id=1, replica_groups=mesh['dom'=8,'sub'=4] {'dom','sub'}, use_global_device_ids=true, to_apply=%region_10.14 | all-reduce | flops 42 | bytes 336 | tf_op jit(solution)/shard_map/psum | solution.py:75
  115.9 1.3 multiply_reduce_fusion.9
  120.5 5.5 %all-gather.1 = f32[4,2,128]{2,1,0:T(2,128)S(1)} all-gather(f32[1,2,128]{2,1,0:T(2,128)S(1)} %bitcast.270), channel_id=1, replica_groups=mesh['dom'=8,'sub'=4] {'sub'}, dimensions={0}, use_global_device_ids=true | all-gather | bytes 5120 | tf_op jit(solution)/shard_map/all_gather | solution.py:33
  126.0 1.3 collective-permute-start.3
  127.2 4.5 %collective-permute-start.2 = (f32[8,128]{1,0:T(8,128)S(1)}, f32[8,128]{1,0:T(8,128)S(1)}, u32[]{:S(2)}, u32[]{:S(2)}) collective-permute-start(f32[8,128]{1,0:T(8,128)S(1)} %bitcast.268), channel_id=1, source_target_pairs={{0,4},{4,8},{8,12},{12,16},{16,20},{20,24},{24,28},{1,5},{5,9},{9,... | collective-permute-start | bytes 12296 | tf_op jit(solution)/shard_map/ppermute | solution.py:16
  135.8 1.0 fusion.62
  137.8 41.0 %all-reduce.3 = (f32[40]{0:T(128)S(1)}, f32[2]{0:T(128)S(1)}, f32[]{:T(128)}) all-reduce(f32[40]{0:T(128)S(1)} %convolution_bitcast_fusion.3, f32[2]{0:T(128)S(1)} %convolution_bitcast_fusion.10, f32[]{:T(128)} %get-tuple-element.127), channel_id=1, replica_groups=mesh['dom'=8,'sub'=4] {'dom','sub'}, use_global_device_ids=true, to_apply=%region_16.20 | all-reduce | flops 43 | bytes 344 | tf_op jit(solution)/shard_map/psum | solution.py:75
  179.7 1.2 multiply_reduce_fusion.8
  182.9 5.5 %all-gather.2 = f32[4,2,128]{2,1,0:T(2,128)S(1)} all-gather(f32[1,2,128]{2,1,0:T(2,128)S(1)} %bitcast.278), channel_id=1, replica_groups=mesh['dom'=8,'sub'=4] {'sub'}, dimensions={0}, use_global_device_ids=true | all-gather | bytes 5120 | tf_op jit(solution)/shard_map/all_gather | solution.py:33
  188.4 1.3 collective-permute-start.5
  189.7 4.5 %collective-permute-start.4 = (f32[8,128]{1,0:T(8,128)S(1)}, f32[8,128]{1,0:T(8,128)S(1)}, u32[]{:S(2)}, u32[]{:S(2)}) collective-permute-start(f32[8,128]{1,0:T(8,128)S(1)} %bitcast.265), channel_id=1, source_target_pairs={{0,4},{4,8},{8,12},{12,16},{16,20},{20,24},{24,28},{1,5},{5,9},{9,... | collective-permute-start | bytes 12296 | tf_op jit(solution)/shard_map/ppermute | solution.py:16
  194.2 1.9 broadcast_select_fusion.6
  196.1 1.3 scatter.34
  199.0 1.0 fusion.63
  200.9 40.7 %all-reduce.2 = (f32[40]{0:T(128)S(1)}, f32[3]{0:T(128)S(1)}, f32[]{:T(128)}) all-reduce(f32[40]{0:T(128)S(1)} %convolution_bitcast_fusion.1, f32[3]{0:T(128)S(1)} %convolution_bitcast_fusion.2, f32[]{:T(128)} %get-tuple-element.125), channel_id=1, replica_groups=mesh['dom'=8,'sub'=4] {'dom','sub'}, use_global_device_ids=true, to_apply=%region_23.27 | all-reduce | flops 44 | bytes 352 | tf_op jit(solution)/shard_map/psum | solution.py:75
  242.1 2.0 broadcast_select_fusion.5
  244.1 1.4 scatter.36
  (109 shorter events, 25.3 us)
Async XLA Ops:
  0.6 72.0 %copy-start = (f32[2,8,128,128]{3,2,1,0:T(8,128)S(1)}, f32[2,8,128,128]{3,2,1,0:T(8,128)}, u32[]{:S(2)}) copy-start(f32[2,8,128,128]{3,2,1,0:T(8,128)} %param.34) | copy-start | bytes 3145732
  2.3 0.7 copy-start.1
  62.0 6.2 %copy-start.3 = (s32[1,4]{1,0:T(1,128)S(1)}, s32[1,4]{1,0:T(1,128)}, u32[]{:S(2)}) copy-start(s32[1,4]{1,0:T(1,128)} %param.36) | copy-start | bytes 52
  62.0 9.4 %collective-permute-start.1 = (f32[8,128]{1,0:T(8,128)S(1)}, f32[8,128]{1,0:T(8,128)S(1)}, u32[]{:S(2)}, u32[]{:S(2)}) collective-permute-start(f32[8,128]{1,0:T(8,128)S(1)} %bitcast.261), channel_id=1, source_target_pairs={{4,0},{8,4},{12,8},{16,12},{20,16},{24,20},{28,24},{5,1},{9,5},{13... | collective-permute-start | bytes 12296 | tf_op jit(solution)/shard_map/ppermute | solution.py:17
  63.4 8.0 %collective-permute-start = (f32[8,128]{1,0:T(8,128)S(1)}, f32[8,128]{1,0:T(8,128)S(1)}, u32[]{:S(2)}, u32[]{:S(2)}) collective-permute-start(f32[8,128]{1,0:T(8,128)S(1)} %bitcast.262), channel_id=1, source_target_pairs={{0,4},{4,8},{8,12},{12,16},{16,20},{20,24},{24,28},{1,5},{5,9},{9,... | collective-permute-start | bytes 12296 | tf_op jit(solution)/shard_map/ppermute | solution.py:16
  68.1 0.7 copy-start.2
  68.9 0.7 copy-start.4
  126.0 8.6 %collective-permute-start.3 = (f32[8,128]{1,0:T(8,128)S(1)}, f32[8,128]{1,0:T(8,128)S(1)}, u32[]{:S(2)}, u32[]{:S(2)}) collective-permute-start(f32[8,128]{1,0:T(8,128)S(1)} %bitcast.267), channel_id=1, source_target_pairs={{4,0},{8,4},{12,8},{16,12},{20,16},{24,20},{28,24},{5,1},{9,5},{13... | collective-permute-start | bytes 12296 | tf_op jit(solution)/shard_map/ppermute | solution.py:17
  127.2 7.3 %collective-permute-start.2 = (f32[8,128]{1,0:T(8,128)S(1)}, f32[8,128]{1,0:T(8,128)S(1)}, u32[]{:S(2)}, u32[]{:S(2)}) collective-permute-start(f32[8,128]{1,0:T(8,128)S(1)} %bitcast.268), channel_id=1, source_target_pairs={{0,4},{4,8},{8,12},{12,16},{16,20},{20,24},{24,28},{1,5},{5,9},{9,... | collective-permute-start | bytes 12296 | tf_op jit(solution)/shard_map/ppermute | solution.py:16
  188.4 9.2 %collective-permute-start.5 = (f32[8,128]{1,0:T(8,128)S(1)}, f32[8,128]{1,0:T(8,128)S(1)}, u32[]{:S(2)}, u32[]{:S(2)}) collective-permute-start(f32[8,128]{1,0:T(8,128)S(1)} %bitcast.264), channel_id=1, source_target_pairs={{4,0},{8,4},{12,8},{16,12},{20,16},{24,20},{28,24},{5,1},{9,5},{13... | collective-permute-start | bytes 12296 | tf_op jit(solution)/shard_map/ppermute | solution.py:17
  189.7 8.0 %collective-permute-start.4 = (f32[8,128]{1,0:T(8,128)S(1)}, f32[8,128]{1,0:T(8,128)S(1)}, u32[]{:S(2)}, u32[]{:S(2)}) collective-permute-start(f32[8,128]{1,0:T(8,128)S(1)} %bitcast.265), channel_id=1, source_target_pairs={{0,4},{4,8},{8,12},{12,16},{16,20},{20,24},{24,28},{1,5},{5,9},{9,... | collective-permute-start | bytes 12296 | tf_op jit(solution)/shard_map/ppermute | solution.py:16
where the time goes:
time: 254 us; the launch traced here: 252 us
  blocking collectives  181 us (71%)
  other arithmetic  26.9 us (11%)
  starting transfers between devices  17.8 us (7%)
  local copies, waits for them, and re-layouts  9.88 us (4%)
  between operations  9.6 us (4%)
  matrix products  7.11 us (3%)
    psum x3, blocking collectives, local(): lax.psum((local_images, jnp.dot(stacked, image_now, precision=highest), j...  122 us
    psum x1, blocking collectives, local(): lax.psum((jnp.dot(images_flat, images_flat.T, precision=highest), jnp.dot...  42.4 us
    all_gather x3, blocking collectives, multiply(): gathered = lax.all_gather(vector, 'sub', axis=0, tiled=True)  16.2 us
    ppermute x3, starting transfers between devices, padded(): before = lax.ppermute(last, axis, up)  13.8 us
    another operation x7, other arithmetic  6.56 us
  transfers between devices with their start and end apart: 6, of which 0 were waited for; matrix products, arithmetic and copies ran while one was open for 3% of the time, Pallas kernels for 0%

commit v1 on v0

--- a/solution.py
+++ b/solution.py
@@ -30,7 +30,12 @@
 def multiply(vector, matrix_tiles, tile_columns, ghost_codes):
     slot_count = vector.shape[0]
     group_size = lax.axis_size("sub") * slot_count
-    gathered = lax.all_gather(vector, "sub", axis=0, tiled=True)
+    ring = [vector]
+    for hop in range(3):
+        ring.append(lax.ppermute(ring[-1], "sub", [(dev, (dev + 1) % 4) for dev in range(4)]))
+    gathered = jnp.roll(
+        jnp.concatenate(ring[::-1], axis=0), (lax.axis_index("sub") + 1) * ring[0].shape[0], axis=0
+    )
     nearby = padded(gathered, (("dom", 0),), group_size)
     ghosts = jnp.take(nearby, ghost_codes, axis=0)
     extended = jnp.concatenate([vector, ghosts], axis=0)

time: 254 us -> 266 us (1.047)
  waiting for transfers between devices: 0.02 us -> 22 us
  blocking collectives: 181 us -> 169 us
    ppermute x0 -> x9, waiting for transfers between devices: none -> 21.3 us  [multiply(): lax.ppermute(ring[-1], 'sub', [(dev, (dev + 1) % 4) for dev in range(4)])]
    all_gather x3 -> x0, blocking collectives: 16.2 us -> none  [multiply(): gathered = lax.all_gather(vector, 'sub', axis=0, tiled=True)]
    psum x3, blocking collectives: 122 us -> 126 us  [local(): lax.psum((local_images, jnp.dot(stacked, image_now, precision=highest), j...]
  transfers between devices with their start and end apart: 6 -> 15, of which waited for: 0 -> 10; matrix products, arithmetic and copies ran while one was open for 3% -> 3% of each run, Pallas kernels for 0% -> 0%
where the time goes in v1:
time: 266 us; the launch traced here: 264 us
  blocking collectives  169 us (64%)
  other arithmetic  27 us (10%)
  waiting for transfers between devices  22 us (8%)
  starting transfers between devices  19.7 us (7%)
  local copies, waits for them, and re-layouts  10.5 us (4%)
  between operations  9.55 us (4%)
  matrix products  7.11 us (3%)
    psum x3, blocking collectives, local(): lax.psum((local_images, jnp.dot(stacked, image_now, precision=highest), j...  126 us
    psum x1, blocking collectives, local(): lax.psum((jnp.dot(images_flat, images_flat.T, precision=highest), jnp.dot...  42.4 us
    ppermute x9, waiting for transfers between devices, multiply(): lax.ppermute(ring[-1], 'sub', [(dev, (dev + 1) % 4) for dev in range(4)])  21.3 us
    ppermute x3, starting transfers between devices, padded(): before = lax.ppermute(last, axis, up)  14.4 us
    another operation x7, other arithmetic  6.5 us
  transfers between devices with their start and end apart: 15, of which 10 were waited for; matrix products, arithmetic and copies ran while one was open for 3% of the time, Pallas kernels for 0%

profile of v1, /device:TPU:0, one launch (start us, length us, event | category | flops | bytes accessed | tf_op | source)
XLA Modules:
  0.0 264.3 jit_solution(1508189952984742930)
XLA Ops:
  3.8 42.4 %all-reduce.5 = (f32[40,40]{0,1:T(8,128)S(1)}, f32[]{:T(128)}, f32[40]{0:T(128)S(1)}) all-reduce(f32[40,40]{0,1:T(8,128)S(1)} %convolution_bitcast_fusion, f32[]{:T(128)} %get-tuple-element.132, f32[40]{0:T(128)S(1)} %convolution_bitcast_fusion.5), channel_id=1, replica_groups=mesh['dom'=8,'sub'=4] {'dom','sub'}, use_global_device_ids=true, to_apply=%region_0.0 | all-reduce | flops 1641 | bytes 13128 | tf_op jit(solution)/shard_map/psum | solution.py:55
  46.3 3.6 %cholesky.29 = f32[40,40]{1,0:T(8,128)S(1)} custom-call(f32[40,40]{1,0:T(8,128)S(1)} %fusion.13), custom_call_target="Cholesky" | custom-call | tf_op jit(solution)/shard_map/jit(cholesky)/cholesky | solution.py:63
  51.3 3.1 %custom-call.17 = f32[1,40,40]{1,2,0:T(8,128)S(1)} custom-call(f32[1,40,40]{2,1,0:T(8,128)S(1)} %fusion.8), custom_call_target="InvertDiagBlocksLowerTriangular" | custom-call | tf_op jit(solution)/shard_map/triangular_solve | solution.py:24
  58.2 1.7 collective-permute-done
  59.9 3.0 %collective-permute-done.1 = f32[2,128]{1,0:T(2,128)S(1)} collective-permute-done((f32[2,128]{1,0:T(2,128)S(1)}, f32[2,128]{1,0:T(2,128)S(1)}, u32[]{:S(2)}, u32[]{:S(2)}) %collective-permute-start.1) | collective-permute-done | bytes 1056 | tf_op jit(solution)/shard_map/ppermute | solution.py:35
  63.0 2.9 %collective-permute-done.2 = f32[2,128]{1,0:T(2,128)S(1)} collective-permute-done((f32[2,128]{1,0:T(2,128)S(1)}, f32[2,128]{1,0:T(2,128)S(1)}, u32[]{:S(2)}, u32[]{:S(2)}) %collective-permute-start.2) | collective-permute-done | bytes 1056 | tf_op jit(solution)/shard_map/ppermute | solution.py:35
  65.9 1.3 collective-permute-start.4
  67.2 4.8 %collective-permute-start.3 = (f32[8,128]{1,0:T(8,128)S(1)}, f32[8,128]{1,0:T(8,128)S(1)}, u32[]{:S(2)}, u32[]{:S(2)}) collective-permute-start(f32[8,128]{1,0:T(8,128)S(1)} %fusion.31), channel_id=1, source_target_pairs={{0,4},{4,8},{8,12},{12,16},{16,20},{20,24},{24,28},{1,5},{5,9},{9,... | collective-permute-start | bytes 12296 | tf_op jit(solution)/shard_map/ppermute | solution.py:16
  77.0 42.7 %all-reduce.4 = (f32[40]{0:T(128)S(1)}, f32[]{:T(128)}, f32[1]{0:T(128)}) all-reduce(f32[40]{0:T(128)S(1)} %convolution_bitcast_fusion.4, f32[]{:T(128)} %multiply_reduce_fusion.3, f32[1]{0:T(128)} %bitcast.27), channel_id=1, replica_groups=mesh['dom'=8,'sub'=4] {'dom','sub'}, use_global_device_ids=true, to_apply=%region_10.15 | all-reduce | flops 42 | bytes 336 | tf_op jit(solution)/shard_map/psum | solution.py:80
  124.5 3.0 %collective-permute-done.5 = f32[2,128]{1,0:T(2,128)S(1)} collective-permute-done((f32[2,128]{1,0:T(2,128)S(1)}, f32[2,128]{1,0:T(2,128)S(1)}, u32[]{:S(2)}, u32[]{:S(2)}) %collective-permute-start.5) | collective-permute-done | bytes 1056 | tf_op jit(solution)/shard_map/ppermute | solution.py:35
  128.0 2.5 collective-permute-done.6
  130.9 2.6 collective-permute-done.7
  133.5 1.3 collective-permute-start.9
  134.8 4.8 %collective-permute-start.8 = (f32[8,128]{1,0:T(8,128)S(1)}, f32[8,128]{1,0:T(8,128)S(1)}, u32[]{:S(2)}, u32[]{:S(2)}) collective-permute-start(f32[8,128]{1,0:T(8,128)S(1)} %fusion.24), channel_id=1, source_target_pairs={{0,4},{4,8},{8,12},{12,16},{16,20},{20,24},{24,28},{1,5},{5,9},{9,... | collective-permute-start | bytes 12296 | tf_op jit(solution)/shard_map/ppermute | solution.py:16
  144.3 42.5 %all-reduce.3 = (f32[40]{0:T(128)S(1)}, f32[2]{0:T(128)S(1)}, f32[]{:T(128)}) all-reduce(f32[40]{0:T(128)S(1)} %convolution_bitcast_fusion.3, f32[2]{0:T(128)S(1)} %convolution_bitcast_fusion.10, f32[]{:T(128)} %get-tuple-element.128), channel_id=1, replica_groups=mesh['dom'=8,'sub'=4] {'dom','sub'}, use_global_device_ids=true, to_apply=%region_16.21 | all-reduce | flops 43 | bytes 344 | tf_op jit(solution)/shard_map/psum | solution.py:80
  191.5 2.4 collective-permute-done.10
  194.2 2.7 %collective-permute-done.11 = f32[2,128]{1,0:T(2,128)S(1)} collective-permute-done((f32[2,128]{1,0:T(2,128)S(1)}, f32[2,128]{1,0:T(2,128)S(1)}, u32[]{:S(2)}, u32[]{:S(2)}) %collective-permute-start.11) | collective-permute-done | bytes 1056 | tf_op jit(solution)/shard_map/ppermute | solution.py:35
  199.9 1.3 collective-permute-start.14
  201.2 4.8 %collective-permute-start.13 = (f32[8,128]{1,0:T(8,128)S(1)}, f32[8,128]{1,0:T(8,128)S(1)}, u32[]{:S(2)}, u32[]{:S(2)}) collective-permute-start(f32[8,128]{1,0:T(8,128)S(1)} %fusion.17), channel_id=1, source_target_pairs={{0,4},{4,8},{8,12},{12,16},{16,20},{20,24},{24,28},{1,5},{5,9},{9,... | collective-permute-start | bytes 12296 | tf_op jit(solution)/shard_map/ppermute | solution.py:16
  206.0 1.9 broadcast_select_fusion.6
  207.9 1.4 scatter.34
  212.6 40.9 %all-reduce.2 = (f32[40]{0:T(128)S(1)}, f32[3]{0:T(128)S(1)}, f32[]{:T(128)}) all-reduce(f32[40]{0:T(128)S(1)} %convolution_bitcast_fusion.1, f32[3]{0:T(128)S(1)} %convolution_bitcast_fusion.2, f32[]{:T(128)} %get-tuple-element.126), channel_id=1, replica_groups=mesh['dom'=8,'sub'=4] {'dom','sub'}, use_global_device_ids=true, to_apply=%region_23.28 | all-reduce | flops 44 | bytes 352 | tf_op jit(solution)/shard_map/psum | solution.py:80
  254.2 2.0 broadcast_select_fusion.5
  256.2 1.4 scatter.36
  (127 shorter events, 33.9 us)
Async XLA Ops:
  0.6 74.0 %copy-start = (f32[2,8,128,128]{3,2,1,0:T(8,128)S(1)}, f32[2,8,128,128]{3,2,1,0:T(8,128)}, u32[]{:S(2)}) copy-start(f32[2,8,128,128]{3,2,1,0:T(8,128)} %param.36) | copy-start | bytes 3145732
  2.3 0.7 copy-start.1
  56.8 0.7 copy-start.2
  56.8 3.1 %collective-permute-start = (f32[2,128]{1,0:T(2,128)S(1)}, f32[2,128]{1,0:T(2,128)S(1)}, u32[]{:S(2)}, u32[]{:S(2)}) collective-permute-start(f32[2,128]{1,0:T(2,128)S(1)} %bitcast.246), channel_id=1, source_target_pairs={{0,1},{1,2},{2,3},{3,0},{4,5},{5,6},{6,7},{7,4},{8,9},{9,10},{10,1... | collective-permute-start | bytes 3080 | tf_op jit(solution)/shard_map/ppermute | solution.py:35
  57.5 0.7 copy-start.3
  59.9 3.0 %collective-permute-start.1 = (f32[2,128]{1,0:T(2,128)S(1)}, f32[2,128]{1,0:T(2,128)S(1)}, u32[]{:S(2)}, u32[]{:S(2)}) collective-permute-start(f32[2,128]{1,0:T(2,128)S(1)} %collective-permute-done), channel_id=1, source_target_pairs={{0,1},{1,2},{2,3},{3,0},{4,5},{5,6},{6,7},{7,4},{8,9},{9,10},{10,1... | collective-permute-start | bytes 3080 | tf_op jit(solution)/shard_map/ppermute | solution.py:35
  62.9 3.0 %collective-permute-start.2 = (f32[2,128]{1,0:T(2,128)S(1)}, f32[2,128]{1,0:T(2,128)S(1)}, u32[]{:S(2)}, u32[]{:S(2)}) collective-permute-start(f32[2,128]{1,0:T(2,128)S(1)} %collective-permute-done.1), channel_id=1, source_target_pairs={{0,1},{1,2},{2,3},{3,0},{4,5},{5,6},{6,7},{7,4},{8,9},{9,10},{10,1... | collective-permute-start | bytes 3080 | tf_op jit(solution)/shard_map/ppermute | solution.py:35
  65.9 6.8 %collective-permute-start.4 = (f32[8,128]{1,0:T(8,128)S(1)}, f32[8,128]{1,0:T(8,128)S(1)}, u32[]{:S(2)}, u32[]{:S(2)}) collective-permute-start(f32[8,128]{1,0:T(8,128)S(1)} %fusion.31), channel_id=1, source_target_pairs={{4,0},{8,4},{12,8},{16,12},{20,16},{24,20},{28,24},{5,1},{9,5},{13... | collective-permute-start | bytes 12296 | tf_op jit(solution)/shard_map/ppermute | solution.py:17
  67.2 6.1 %collective-permute-start.3 = (f32[8,128]{1,0:T(8,128)S(1)}, f32[8,128]{1,0:T(8,128)S(1)}, u32[]{:S(2)}, u32[]{:S(2)}) collective-permute-start(f32[8,128]{1,0:T(8,128)S(1)} %fusion.31), channel_id=1, source_target_pairs={{0,4},{4,8},{8,12},{12,16},{16,20},{20,24},{24,28},{1,5},{5,9},{9,... | collective-permute-start | bytes 12296 | tf_op jit(solution)/shard_map/ppermute | solution.py:16
  124.4 3.1 %collective-permute-start.5 = (f32[2,128]{1,0:T(2,128)S(1)}, f32[2,128]{1,0:T(2,128)S(1)}, u32[]{:S(2)}, u32[]{:S(2)}) collective-permute-start(f32[2,128]{1,0:T(2,128)S(1)} %bitcast.256), channel_id=1, source_target_pairs={{0,1},{1,2},{2,3},{3,0},{4,5},{5,6},{6,7},{7,4},{8,9},{9,10},{10,1... | collective-permute-start | bytes 3080 | tf_op jit(solution)/shard_map/ppermute | solution.py:35
  127.5 3.0 %collective-permute-start.6 = (f32[2,128]{1,0:T(2,128)S(1)}, f32[2,128]{1,0:T(2,128)S(1)}, u32[]{:S(2)}, u32[]{:S(2)}) collective-permute-start(f32[2,128]{1,0:T(2,128)S(1)} %collective-permute-done.5), channel_id=1, source_target_pairs={{0,1},{1,2},{2,3},{3,0},{4,5},{5,6},{6,7},{7,4},{8,9},{9,10},{10,1... | collective-permute-start | bytes 3080 | tf_op jit(solution)/shard_map/ppermute | solution.py:35
  130.5 3.0 %collective-permute-start.7 = (f32[2,128]{1,0:T(2,128)S(1)}, f32[2,128]{1,0:T(2,128)S(1)}, u32[]{:S(2)}, u32[]{:S(2)}) collective-permute-start(f32[2,128]{1,0:T(2,128)S(1)} %collective-permute-done.6), channel_id=1, source_target_pairs={{0,1},{1,2},{2,3},{3,0},{4,5},{5,6},{6,7},{7,4},{8,9},{9,10},{10,1... | collective-permute-start | bytes 3080 | tf_op jit(solution)/shard_map/ppermute | solution.py:35
  130.9 8.7 %copy-start.4 = (s32[2]{0:T(128)S(1)}, s32[2]{0:T(128)}, u32[]{:S(2)}) copy-start(s32[2]{0:T(128)} %constant.360.clone.1) | copy-start | bytes 28
  133.5 7.5 %collective-permute-start.9 = (f32[8,128]{1,0:T(8,128)S(1)}, f32[8,128]{1,0:T(8,128)S(1)}, u32[]{:S(2)}, u32[]{:S(2)}) collective-permute-start(f32[8,128]{1,0:T(8,128)S(1)} %fusion.24), channel_id=1, source_target_pairs={{4,0},{8,4},{12,8},{16,12},{20,16},{24,20},{28,24},{5,1},{9,5},{13... | collective-permute-start | bytes 12296 | tf_op jit(solution)/shard_map/ppermute | solution.py:17
  134.8 6.2 %collective-permute-start.8 = (f32[8,128]{1,0:T(8,128)S(1)}, f32[8,128]{1,0:T(8,128)S(1)}, u32[]{:S(2)}, u32[]{:S(2)}) collective-permute-start(f32[8,128]{1,0:T(8,128)S(1)} %fusion.24), channel_id=1, source_target_pairs={{0,4},{4,8},{8,12},{12,16},{16,20},{20,24},{24,28},{1,5},{5,9},{9,... | collective-permute-start | bytes 12296 | tf_op jit(solution)/shard_map/ppermute | solution.py:16
  190.8 3.1 %collective-permute-start.10 = (f32[2,128]{1,0:T(2,128)S(1)}, f32[2,128]{1,0:T(2,128)S(1)}, u32[]{:S(2)}, u32[]{:S(2)}) collective-permute-start(f32[2,128]{1,0:T(2,128)S(1)} %bitcast.265), channel_id=1, source_target_pairs={{0,1},{1,2},{2,3},{3,0},{4,5},{5,6},{6,7},{7,4},{8,9},{9,10},{10,1... | collective-permute-start | bytes 3080 | tf_op jit(solution)/shard_map/ppermute | solution.py:35
  193.8 3.0 %collective-permute-start.11 = (f32[2,128]{1,0:T(2,128)S(1)}, f32[2,128]{1,0:T(2,128)S(1)}, u32[]{:S(2)}, u32[]{:S(2)}) collective-permute-start(f32[2,128]{1,0:T(2,128)S(1)} %collective-permute-done.10), channel_id=1, source_target_pairs={{0,1},{1,2},{2,3},{3,0},{4,5},{5,6},{6,7},{7,4},{8,9},{9,10},{10,1... | collective-permute-start | bytes 3080 | tf_op jit(solution)/shard_map/ppermute | solution.py:35
  196.8 3.0 %collective-permute-start.12 = (f32[2,128]{1,0:T(2,128)S(1)}, f32[2,128]{1,0:T(2,128)S(1)}, u32[]{:S(2)}, u32[]{:S(2)}) collective-permute-start(f32[2,128]{1,0:T(2,128)S(1)} %collective-permute-done.11), channel_id=1, source_target_pairs={{0,1},{1,2},{2,3},{3,0},{4,5},{5,6},{6,7},{7,4},{8,9},{9,10},{10,1... | collective-permute-start | bytes 3080 | tf_op jit(solution)/shard_map/ppermute | solution.py:35
  199.9 9.5 %collective-permute-start.14 = (f32[8,128]{1,0:T(8,128)S(1)}, f32[8,128]{1,0:T(8,128)S(1)}, u32[]{:S(2)}, u32[]{:S(2)}) collective-permute-start(f32[8,128]{1,0:T(8,128)S(1)} %fusion.17), channel_id=1, source_target_pairs={{4,0},{8,4},{12,8},{16,12},{20,16},{24,20},{28,24},{5,1},{9,5},{13... | collective-permute-start | bytes 12296 | tf_op jit(solution)/shard_map/ppermute | solution.py:17
  201.2 8.2 %collective-permute-start.13 = (f32[8,128]{1,0:T(8,128)S(1)}, f32[8,128]{1,0:T(8,128)S(1)}, u32[]{:S(2)}, u32[]{:S(2)}) collective-permute-start(f32[8,128]{1,0:T(8,128)S(1)} %fusion.17), channel_id=1, source_target_pairs={{0,4},{4,8},{8,12},{12,16},{16,20},{20,24},{24,28},{1,5},{5,9},{9,... | collective-permute-start | bytes 12296 | tf_op jit(solution)/shard_map/ppermute | solution.py:16
